TPU v7x, 32 devices: a whole 2x2x4 slice. The times are simulated.
32 devices in a mesh: dp: 4 (over y, x), seq: 8 (over z, core).
Axes of the slice: x: 2, y: 2, z: 4, core: 2. Of those that a mesh axis runs over, the one named last changes fastest.
Arguments:
- queries: bfloat16 [4, 1024, 2048], P('dp', 'seq'), may hold values from -6 to 6
- key_vectors: bfloat16 [4, 1024, 2048], P('dp', 'seq'), may hold values from -6 to 6
- values: bfloat16 [4, 1024, 2048], P('dp', 'seq'), may hold values from -6 to 6
- out_grad: bfloat16 [4, 1024, 2048], P('dp', 'seq'), may hold values from -6 to 6
- inputs: bfloat16 [4, 1024, 2048], P('dp', 'seq'), may hold values from -6 to 6
Outputs:
- query_grad: bfloat16 [4, 1024, 2048], P('dp', 'seq')
- key_grad: bfloat16 [4, 1024, 2048], P('dp', 'seq')
- value_grad: bfloat16 [4, 1024, 2048], P('dp', 'seq')
- weight_grad: float32 [2048, 2048], P('dp', 'seq')
All inputs are finite; a program needn't handle non-finite values.
Results may differ from a plain program's by a relative error of at most 0.025.
Values may be sent and summed in bfloat16 or wider, within the bound.
No kernel may reach another device: no remote copies, remote signals or barrier semaphores. Data moves between devices by JAX's collectives and lax.ppermute only.
A program may use at most 128 MiB of HBM per device.

v0:
```python
import jax
import jax.numpy as jnp
from jax import lax
from jax.sharding import PartitionSpec as P

HD = 128


def partner(value, axis, apart):
    return lax.ppermute(value, axis, [(i, i ^ 1 << apart) for i in range(lax.axis_size(axis))])


def body(queries, key_vectors, values, out_grad, inputs):
    seq_count = lax.axis_size("seq")
    groups = seq_count // 2
    parity = lax.axis_index("seq") % 2
    is_even = parity == 0
    tok_rows = queries.shape[1]
    half_rows = tok_rows // 2
    width = queries.shape[2]
    group_width = 2 * width // seq_count
    heads_here = group_width // HD
    model_width = inputs.shape[2]
    own_rows = seq_count * half_rows
    length = 2 * own_rows
    doc_rows = own_rows // 4
    block_rows = min(doc_rows, max(256, length // 16))
    block_count = own_rows // block_rows
    scale = HD ** (-0.5)

    def to_heads(array):
        return (
            array[0]
            .reshape(half_rows, 2, groups, group_width)
            .transpose(0, 2, 1, 3)
            .reshape(half_rows, seq_count, group_width)
        )

    moved = (
        lax.all_to_all(to_heads(queries), "seq", split_axis=1, concat_axis=0, tiled=True),
        lax.all_to_all(to_heads(key_vectors), "seq", split_axis=1, concat_axis=0, tiled=True),
        lax.all_to_all(to_heads(values), "seq", split_axis=1, concat_axis=0, tiled=True),
        lax.all_to_all(to_heads(out_grad), "seq", split_axis=1, concat_axis=0, tiled=True),
    )
    q_rows = moved[0].reshape(own_rows, group_width)
    k_rows = moved[1].reshape(own_rows, group_width)
    v_rows = moved[2].reshape(own_rows, group_width)
    g_rows = moved[3].reshape(own_rows, group_width)
    k_other, v_other = partner((k_rows, v_rows), "seq", 0)

    def in_order(mine, theirs):
        even_rows = jnp.where(is_even, mine, theirs)
        odd_rows = jnp.where(is_even, theirs, mine)
        return jnp.stack([even_rows, odd_rows], axis=1).reshape(2 * mine.shape[0], mine.shape[1])

    key_all = in_order(k_rows, k_other).reshape(length, heads_here, HD)
    value_all = in_order(v_rows, v_other).reshape(length, heads_here, HD)
    query_heads = q_rows.reshape(own_rows, heads_here, HD)
    grad_heads = g_rows.reshape(own_rows, heads_here, HD)
    key_total = jnp.zeros((length, heads_here, HD), jnp.float32)
    value_total = jnp.zeros((length, heads_here, HD), jnp.float32)
    query_parts = []
    for block in range(block_count):
        start = block * block_rows
        stop = start + block_rows
        low = 2 * (start // doc_rows * doc_rows)
        high = 2 * stop
        query_block = query_heads[start:stop]
        grad_block = grad_heads[start:stop]
        key_block = key_all[low:high]
        value_block = value_all[low:high]
        scores = (
            jnp.einsum("qhd,khd->hqk", query_block, key_block, preferred_element_type=jnp.float32)
            * scale
        )
        query_pos = 2 * (start + jnp.arange(block_rows, dtype=jnp.int32)) + parity
        key_pos = low + jnp.arange(high - low, dtype=jnp.int32)
        visible = key_pos[None, :] <= query_pos[:, None]
        scores = jnp.where(visible[None], scores, -jnp.inf)
        top = jnp.max(scores, axis=2, keepdims=True)
        weights = jnp.exp(scores - top)
        probs = weights / jnp.sum(weights, axis=2, keepdims=True)
        probs_low = probs.astype(jnp.bfloat16)
        dprob = jnp.einsum(
            "qhd,khd->hqk", grad_block, value_block, preferred_element_type=jnp.float32
        )
        delta = jnp.sum(probs * dprob, axis=2, keepdims=True)
        dscore = (probs * (dprob - delta) * scale).astype(jnp.bfloat16)
        query_parts.append(
            jnp.einsum(
                "hqk,khd->qhd", dscore, key_block, preferred_element_type=jnp.float32
            ).astype(jnp.bfloat16)
        )
        key_total = key_total.at[low:high].add(
            jnp.einsum("hqk,qhd->khd", dscore, query_block, preferred_element_type=jnp.float32)
        )
        value_total = value_total.at[low:high].add(
            jnp.einsum("hqk,qhd->khd", probs_low, grad_block, preferred_element_type=jnp.float32)
        )
    query_grad = jnp.concatenate(query_parts, axis=0).reshape(own_rows, group_width)

    def by_parity(total):
        paired = total.reshape(own_rows, 2, group_width)
        mine = jnp.where(is_even, paired[:, 0], paired[:, 1])
        theirs = jnp.where(is_even, paired[:, 1], paired[:, 0])
        return (mine.astype(jnp.bfloat16), theirs.astype(jnp.bfloat16))

    key_mine, key_theirs = by_parity(key_total)
    value_mine, value_theirs = by_parity(value_total)
    key_back, value_back = partner((key_theirs, value_theirs), "seq", 0)
    key_grad = (key_mine.astype(jnp.float32) + key_back.astype(jnp.float32)).astype(jnp.bfloat16)
    value_grad = (value_mine.astype(jnp.float32) + value_back.astype(jnp.float32)).astype(
        jnp.bfloat16
    )
    spread = jnp.broadcast_to(
        inputs[0].reshape(half_rows, 1, 2, model_width), (half_rows, groups, 2, model_width)
    ).reshape(half_rows, seq_count, model_width)
    input_rows = lax.all_to_all(spread, "seq", split_axis=1, concat_axis=0, tiled=True).reshape(
        own_rows, model_width
    )
    term = jnp.einsum("td,tc->dc", input_rows, value_grad, preferred_element_type=jnp.float32)
    halves = term.reshape(term.shape[0], 2, term.shape[1] // 2)
    mine = jnp.where(is_even, halves[:, 0], halves[:, 1])
    theirs = jnp.where(is_even, halves[:, 1], halves[:, 0])
    mine, theirs = (mine, theirs)
    received = partner(theirs.astype(jnp.bfloat16), "seq", 0).astype(theirs.dtype)
    weight_grad = lax.psum_scatter(
        (mine + received).astype(jnp.bfloat16), "dp", scatter_dimension=0, tiled=True
    ).astype(jnp.float32)

    def to_tokens(array):
        return array.reshape(seq_count, half_rows, 1, group_width)

    def from_heads(array):
        return (
            array.reshape(half_rows, groups, 2, group_width)
            .transpose(0, 2, 1, 3)
            .reshape(1, tok_rows, width)
        )

    returned = (
        lax.all_to_all(to_tokens(query_grad), "seq", split_axis=0, concat_axis=2, tiled=True),
        lax.all_to_all(to_tokens(key_grad), "seq", split_axis=0, concat_axis=2, tiled=True),
        lax.all_to_all(to_tokens(value_grad), "seq", split_axis=0, concat_axis=2, tiled=True),
    )
    return (from_heads(returned[0]), from_heads(returned[1]), from_heads(returned[2]), weight_grad)


def solution(mesh):
    return jax.shard_map(
        body,
        mesh=mesh,
        in_specs=(
            P("dp", "seq", None),
            P("dp", "seq", None),
            P("dp", "seq", None),
            P("dp", "seq", None),
            P("dp", "seq", None),
        ),
        out_specs=(
            P("dp", "seq", None),
            P("dp", "seq", None),
            P("dp", "seq", None),
            P("dp", "seq"),
        ),
        check_vma=False,
    )
```

profile of v0, /device:TPU:0, one launch (start us, length us, event | category | flops | bytes accessed | tf_op | source)
XLA Modules:
  0.0 255.6 jit_solution(17739342030090548654)
XLA Ops:
  9.6 6.5 %all-to-all-start.2 = ((bf16[64,8,512]{2,0,1:T(8,128)(2,1)}), bf16[64,8,512]{2,0,1:T(8,128)(2,1)S(1)}, u32[]{:S(2)}, u32[]{:S(2)}) async-start(bf16[64,8,512]{2,0,1:T(8,128)(2,1)} %bitcast.15), calls=%async_computation.2 | async-start | bytes 1048576 | tf_op jit(solution)/shard_map/all_to_all | solution.py:42
  17.4 14.0 %all-to-all-done.2 = bf16[64,8,512]{2,0,1:T(8,128)(2,1)S(1)} async-done(((bf16[64,8,512]{2,0,1:T(8,128)(2,1)}), bf16[64,8,512]{2,0,1:T(8,128)(2,1)S(1)}, u32[]{:S(2)}, u32[]{:S(2)}) %all-to-all-start.2) | async-done | bytes 524320 | tf_op jit(solution)/shard_map/all_to_all | solution.py:42
  31.4 3.6 %all-to-all-start.3 = ((bf16[64,8,512]{2,0,1:T(8,128)(2,1)}), bf16[64,8,512]{2,0,1:T(8,128)(2,1)S(1)}, u32[]{:S(2)}, u32[]{:S(2)}) async-start(bf16[64,8,512]{2,0,1:T(8,128)(2,1)} %bitcast.24), calls=%async_computation.3 | async-start | bytes 1048576 | tf_op jit(solution)/shard_map/all_to_all | solution.py:43
  36.4 13.9 %all-to-all-done.3 = bf16[64,8,512]{2,0,1:T(8,128)(2,1)S(1)} async-done(((bf16[64,8,512]{2,0,1:T(8,128)(2,1)}), bf16[64,8,512]{2,0,1:T(8,128)(2,1)S(1)}, u32[]{:S(2)}, u32[]{:S(2)}) %all-to-all-start.3) | async-done | bytes 524320 | tf_op jit(solution)/shard_map/all_to_all | solution.py:43
  50.4 3.5 %all-to-all-start = ((bf16[64,8,512]{2,0,1:T(8,128)(2,1)}), bf16[64,8,512]{2,0,1:T(8,128)(2,1)S(1)}, u32[]{:S(2)}, u32[]{:S(2)}) async-start(bf16[64,8,512]{2,0,1:T(8,128)(2,1)} %bitcast.1), calls=%async_computation | async-start | bytes 1048576 | tf_op jit(solution)/shard_map/all_to_all | solution.py:41
  55.9 13.2 %all-to-all-done = bf16[64,8,512]{2,0,1:T(8,128)(2,1)S(1)} async-done(((bf16[64,8,512]{2,0,1:T(8,128)(2,1)}), bf16[64,8,512]{2,0,1:T(8,128)(2,1)S(1)}, u32[]{:S(2)}, u32[]{:S(2)}) %all-to-all-start) | async-done | bytes 524320 | tf_op jit(solution)/shard_map/all_to_all | solution.py:41
  69.1 3.5 %all-to-all-start.1 = ((bf16[64,8,512]{2,0,1:T(8,128)(2,1)}), bf16[64,8,512]{2,0,1:T(8,128)(2,1)S(1)}, u32[]{:S(2)}, u32[]{:S(2)}) async-start(bf16[64,8,512]{2,0,1:T(8,128)(2,1)} %bitcast.10), calls=%async_computation.1 | async-start | bytes 1048576 | tf_op jit(solution)/shard_map/all_to_all | solution.py:40
  77.6 10.3 %all-to-all-done.1 = bf16[64,8,512]{2,0,1:T(8,128)(2,1)S(1)} async-done(((bf16[64,8,512]{2,0,1:T(8,128)(2,1)}), bf16[64,8,512]{2,0,1:T(8,128)(2,1)S(1)}, u32[]{:S(2)}, u32[]{:S(2)}) %all-to-all-start.1) | async-done | bytes 524320 | tf_op jit(solution)/shard_map/all_to_all | solution.py:40
  89.5 3.8 %all-to-all-start.7 = ((bf16[64,8,2048]{2,0,1:T(8,128)(2,1)}), bf16[64,8,2048]{2,0,1:T(8,128)(2,1)S(1)}, u32[]{:S(2)}, u32[]{:S(2)}) async-start(bf16[64,8,2048]{2,0,1:T(8,128)(2,1)} %bitcast.65), calls=%async_computation.7 | async-start | bytes 4194304 | tf_op jit(solution)/shard_map/all_to_all | solution.py:118
  136.2 3.9 %copy.167 = bf16[1024,4,128]{2,1,0:T(4,128)(2,1)} copy(f32[1024,4,128]{2,0,1:T(8,128)} %fusion.26) | data formatting | bytes 3145728 | tf_op jit(solution)/shard_map/scatter-add | solution.py:97
  141.6 3.0 %fusion.60 = (bf16[512,1,512]{2,1,0:T(2,128)(2,1)S(1)}, f32[512,1,512]{2,1,0:T(1,128)}) fusion(pred[]{:T(512)S(6)} %eq.5, bf16[512,2,512]{2,1,0:T(2,128)(2,1)S(1)} %reshape.498), kind=kLoop, calls=%fused_computation.98 | loop fusion | flops 786432 | bytes 2621441 | tf_op jit(solution)/shard_map/convert_element_type | solution.py:106
  150.4 2.7 %fusion.53 = bf16[128,4,128]{2,0,1:T(8,128)(2,1)} fusion(f32[4,128,256]{1,2,0:T(8,128)} %convolution_bitcast_fusion.9, bf16[256,4,128]{2,1,0:T(4,128)(2,1)} %copy-done.18, f32[4,128,256]{1,2,0:T(8,128)} %get-tuple-element.129, f32[4,128]{1,0:T(4,128)S(1)} %get-tuple-element.128), kind=kOutput, calls=%fused_computation.91 | convolution fusion | flops 34538240 | bytes 1443840 | tf_op jit(solution)/shard_map/hqk,khd->qhd/dot_general | solution.py:90
  154.2 2.7 %fusion.52 = bf16[128,4,128]{2,0,1:T(8,128)(2,1)} fusion(f32[4,128,256]{1,2,0:T(8,128)} %convolution_bitcast_fusion.10, bf16[256,4,128]{2,1,0:T(4,128)(2,1)} %slice.311, f32[4,128,256]{1,2,0:T(8,128)} %get-tuple-element.131, f32[4,128]{1,0:T(4,128)S(1)} %get-tuple-element.130), kind=kOutput, calls=%fused_computation.90 | convolution fusion | flops 34538240 | bytes 1443840 | tf_op jit(solution)/shard_map/hqk,khd->qhd/dot_general | solution.py:90
  165.3 2.8 %fusion.18 = f32[1024,4,128]{2,0,1:T(8,128)} fusion(f32[1024,4,128]{2,0,1:T(8,128)} %scatter-add.26, f32[4,128,256]{1,2,0:T(8,128)} %convolution_bitcast_fusion.10, bf16[128,4,128]{2,1,0:T(4,128)(2,1)S(1)} %copy-done.23, f32[4,128,256]{1,2,0:T(8,128)} %get-tuple-element.131, f32[4,128]{1,0:T(4,128)S(1)} %get-tuple-element.130), kind=kOutput, calls=%fused_computation.43 | convolution fusion | flops 34472704 | bytes 2756608 | tf_op jit(solution)/shard_map/hqk,qhd->khd/dot_general | solution.py:95
  170.1 4.8 %all-to-all-start.4 = ((bf16[8,64,1,512]{3,1,2,0:T(8,128)(2,1)}), bf16[8,64,1,512]{3,1,2,0:T(8,128)(2,1)}, u32[]{:S(2)}, u32[]{:S(2)}) async-start(bf16[8,64,1,512]{3,1,2,0:T(8,128)(2,1)} %bitcast.239), calls=%async_computation.4 | async-start | bytes 1048576 | tf_op jit(solution)/shard_map/all_to_all | solution.py:142
  181.4 2.9 %copy.181 = f32[2048,1,256]{2,0,1:T(8,128)} copy(f32[2048,1,256]{0,2,1:T(8,128)} %get-tuple-element.100) | data formatting | bytes 4194304
  187.7 2.8 %fusion.20 = f32[1024,4,128]{2,0,1:T(8,128)} fusion(f32[1024,4,128]{2,0,1:T(8,128)} %fusion.18, f32[4,128,256]{1,2,0:T(8,128)} %convolution_bitcast_fusion.9, bf16[128,4,128]{2,1,0:T(4,128)(2,1)S(1)} %copy-done.22, f32[4,128,256]{1,2,0:T(8,128)} %get-tuple-element.129, f32[4,128]{1,0:T(4,128)S(1)} %get-tuple-element.128), kind=kOutput, calls=%fused_computation.50 | convolution fusion | flops 34603776 | bytes 3280896 | tf_op jit(solution)/shard_map/hqk,qhd->khd/dot_general | solution.py:95
  190.5 2.8 %fusion.22 = f32[1024,4,128]{2,0,1:T(8,128)} fusion(f32[1024,4,128]{2,0,1:T(8,128)} %fusion.20, f32[4,128,256]{1,2,0:T(8,128)} %copy-done.7, bf16[128,4,128]{2,1,0:T(4,128)(2,1)S(1)} %copy-done.20, f32[4,128,256]{1,2,0:T(8,128)} %get-tuple-element.127, f32[4,128]{1,0:T(4,128)S(1)} %get-tuple-element.126), kind=kOutput, calls=%fused_computation.52 | convolution fusion | flops 34603776 | bytes 3280896 | tf_op jit(solution)/shard_map/hqk,qhd->khd/dot_general | solution.py:95
  193.3 3.9 %copy.160 = bf16[1024,4,128]{2,1,0:T(4,128)(2,1)} copy(f32[1024,4,128]{2,0,1:T(8,128)} %fusion.22) | data formatting | bytes 3145728 | tf_op jit(solution)/shard_map/scatter-add | solution.py:94
  198.7 3.0 %fusion.57 = (bf16[512,1,512]{2,1,0:T(2,128)(2,1)S(1)}, f32[512,1,512]{2,1,0:T(1,128)}) fusion(pred[]{:T(512)S(6)} %eq.5, bf16[512,2,512]{2,1,0:T(2,128)(2,1)S(1)} %reshape.494), kind=kLoop, calls=%fused_computation.95 | loop fusion | flops 786432 | bytes 2621441 | tf_op jit(solution)/shard_map/convert_element_type | solution.py:106
  202.7 2.7 %fusion.8 = bf16[2048,256]{1,0:T(8,128)(2,1)} fusion(bf16[2048,256]{1,0:T(8,128)(2,1)} %collective-permute-done.4, f32[2048,1,256]{2,0,1:T(8,128)S(1)} %copy-done, f32[2048,1,256]{2,0,1:T(8,128)S(1)} %copy.182, pred[]{:T(512)S(6)} %eq.5), kind=kLoop, calls=%fused_computation.9 | loop fusion | flops 2097152 | bytes 6291457 | tf_op jit(solution)/shard_map/convert_element_type | solution.py:128
  206.7 19.9 %all_to_all.120 = bf16[8,64,1,512]{3,1,2,0:T(8,128)(2,1)S(1)} all-to-all(bf16[8,64,1,512]{3,1,2,0:T(8,128)(2,1)S(1)} %bitcast.248), channel_id=1, replica_groups=mesh['dp'=4,'seq'=8] {'seq'}, dimensions={0} | all-to-all | bytes 1048576 | tf_op jit(solution)/shard_map/all_to_all | solution.py:143
  226.6 3.8 %all-to-all-start.6 = ((bf16[8,64,1,512]{3,1,2,0:T(8,128)(2,1)}), bf16[8,64,1,512]{3,1,2,0:T(8,128)(2,1)S(1)}, u32[]{:S(2)}, u32[]{:S(2)}) async-start(bf16[8,64,1,512]{3,1,2,0:T(8,128)(2,1)} %bitcast.60), calls=%async_computation.6 | async-start | bytes 1048576 | tf_op jit(solution)/shard_map/all_to_all | solution.py:144
  234.6 10.8 %all-to-all-done.6 = bf16[8,64,1,512]{3,1,2,0:T(8,128)(2,1)S(1)} async-done(((bf16[8,64,1,512]{3,1,2,0:T(8,128)(2,1)}), bf16[8,64,1,512]{3,1,2,0:T(8,128)(2,1)S(1)}, u32[]{:S(2)}, u32[]{:S(2)}) %all-to-all-start.6) | async-done | bytes 524320 | tf_op jit(solution)/shard_map/all_to_all | solution.py:144
  (158 shorter events, 96.1 us)
Async XLA Ops:
  7.2 8.9 %copy-start.12 = (bf16[1,128,2048]{2,1,0:T(8,128)(2,1)S(1)}, bf16[1,128,2048]{2,1,0:T(8,128)(2,1)}, u32[]{:S(2)}) copy-start(bf16[1,128,2048]{2,1,0:T(8,128)(2,1)} %param.24) | copy-start | bytes 1572868
  9.6 25.5 %copy-start.13 = (bf16[1,128,2048]{2,1,0:T(8,128)(2,1)S(1)}, bf16[1,128,2048]{2,1,0:T(8,128)(2,1)}, u32[]{:S(2)}) copy-start(bf16[1,128,2048]{2,1,0:T(8,128)(2,1)} %param.22) | copy-start | bytes 1572868
  9.6 21.8 %all-to-all-start.2 = ((bf16[64,8,512]{2,0,1:T(8,128)(2,1)}), bf16[64,8,512]{2,0,1:T(8,128)(2,1)S(1)}, u32[]{:S(2)}, u32[]{:S(2)}) async-start(bf16[64,8,512]{2,0,1:T(8,128)(2,1)} %bitcast.15), calls=%async_computation.2 | async-start | bytes 1048576 | tf_op jit(solution)/shard_map/all_to_all | solution.py:42
  31.4 22.4 %copy-start.14 = (bf16[1,128,2048]{2,1,0:T(8,128)(2,1)S(1)}, bf16[1,128,2048]{2,1,0:T(8,128)(2,1)}, u32[]{:S(2)}) copy-start(bf16[1,128,2048]{2,1,0:T(8,128)(2,1)} %param.21) | copy-start | bytes 1572868
  31.4 18.9 %all-to-all-start.3 = ((bf16[64,8,512]{2,0,1:T(8,128)(2,1)}), bf16[64,8,512]{2,0,1:T(8,128)(2,1)S(1)}, u32[]{:S(2)}, u32[]{:S(2)}) async-start(bf16[64,8,512]{2,0,1:T(8,128)(2,1)} %bitcast.24), calls=%async_computation.3 | async-start | bytes 1048576 | tf_op jit(solution)/shard_map/all_to_all | solution.py:43
  50.4 18.8 %all-to-all-start = ((bf16[64,8,512]{2,0,1:T(8,128)(2,1)}), bf16[64,8,512]{2,0,1:T(8,128)(2,1)S(1)}, u32[]{:S(2)}, u32[]{:S(2)}) async-start(bf16[64,8,512]{2,0,1:T(8,128)(2,1)} %bitcast.1), calls=%async_computation | async-start | bytes 1048576 | tf_op jit(solution)/shard_map/all_to_all | solution.py:41
  69.1 18.8 %all-to-all-start.1 = ((bf16[64,8,512]{2,0,1:T(8,128)(2,1)}), bf16[64,8,512]{2,0,1:T(8,128)(2,1)S(1)}, u32[]{:S(2)}, u32[]{:S(2)}) async-start(bf16[64,8,512]{2,0,1:T(8,128)(2,1)} %bitcast.10), calls=%async_computation.1 | async-start | bytes 1048576 | tf_op jit(solution)/shard_map/all_to_all | solution.py:40
  74.1 30.5 %collective-permute-start = (bf16[512,512]{1,0:T(8,128)(2,1)S(1)}, bf16[512,512]{1,0:T(8,128)(2,1)}, u32[]{:S(2)}, u32[]{:S(2)}) collective-permute-start(bf16[512,512]{1,0:T(8,128)(2,1)S(1)} %bitcast.238), channel_id=1, source_target_pairs={{0,1},{1,0},{2,3},{3,2},{4,5},{5,4},{6,7},{7,6},{8,9},{9,8},{10,11... | collective-permute-start | bytes 1572872 | tf_op jit(solution)/shard_map/ppermute | solution.py:10
  76.6 51.8 %collective-permute-start.1 = (bf16[512,512]{1,0:T(8,128)(2,1)S(1)}, bf16[512,512]{1,0:T(8,128)(2,1)}, u32[]{:S(2)}, u32[]{:S(2)}) collective-permute-start(bf16[512,512]{1,0:T(8,128)(2,1)S(1)} %bitcast.237), channel_id=1, source_target_pairs={{0,1},{1,0},{2,3},{3,2},{4,5},{5,4},{6,7},{7,6},{8,9},{9,8},{10,11... | collective-permute-start | bytes 1572872 | tf_op jit(solution)/shard_map/ppermute | solution.py:10
  89.5 80.6 %all-to-all-start.7 = ((bf16[64,8,2048]{2,0,1:T(8,128)(2,1)}), bf16[64,8,2048]{2,0,1:T(8,128)(2,1)S(1)}, u32[]{:S(2)}, u32[]{:S(2)}) async-start(bf16[64,8,2048]{2,0,1:T(8,128)(2,1)} %bitcast.65), calls=%async_computation.7 | async-start | bytes 4194304 | tf_op jit(solution)/shard_map/all_to_all | solution.py:118
  110.1 6.9 %copy-start.15 = (bf16[256,4,128]{2,1,0:T(4,128)(2,1)}, bf16[256,4,128]{2,1,0:T(4,128)(2,1)S(1)}, u32[]{:S(2)}) copy-start(bf16[256,4,128]{2,1,0:T(4,128)(2,1)S(1)} %slice.303) | copy-start | bytes 786436
  112.3 4.8 %copy-start.19 = (bf16[128,4,128]{2,1,0:T(4,128)(2,1)S(1)}, bf16[128,4,128]{2,1,0:T(4,128)(2,1)}, u32[]{:S(2)}) copy-start(bf16[128,4,128]{2,1,0:T(4,128)(2,1)} %slice.329) | copy-start | bytes 393220
  121.4 4.7 %copy-start.11 = (bf16[128,4,128]{2,1,0:T(4,128)(2,1)S(1)}, bf16[128,4,128]{2,1,0:T(4,128)(2,1)}, u32[]{:S(2)}) copy-start(bf16[128,4,128]{2,1,0:T(4,128)(2,1)} %slice.325) | copy-start | bytes 393220
  145.5 22.5 %collective-permute-start.3 = (bf16[512,512]{1,0:T(8,128)(2,1)}, bf16[512,512]{1,0:T(8,128)(2,1)}, u32[]{:S(2)}, u32[]{:S(2)}) collective-permute-start(bf16[512,512]{1,0:T(8,128)(2,1)} %bitcast.233), channel_id=1, source_target_pairs={{0,1},{1,0},{2,3},{3,2},{4,5},{5,4},{6,7},{7,6},{8,9},{9,8},{10,11... | collective-permute-start | bytes 1572872 | tf_op jit(solution)/shard_map/ppermute | solution.py:10
  146.0 7.2 %copy-start.7 = (f32[4,128,256]{1,2,0:T(8,128)}, f32[4,128,256]{1,2,0:T(8,128)S(1)}, u32[]{:S(2)}) copy-start(f32[4,128,256]{1,2,0:T(8,128)S(1)} %convolution_bitcast_fusion.8) | copy-start | bytes 1572868
  148.5 4.7 %copy-start.10 = (bf16[128,4,128]{2,1,0:T(4,128)(2,1)S(1)}, bf16[128,4,128]{2,1,0:T(4,128)(2,1)}, u32[]{:S(2)}) copy-start(bf16[128,4,128]{2,1,0:T(4,128)(2,1)} %slice.317) | copy-start | bytes 393220
  160.3 5.0 %copy-start.23 = (bf16[128,4,128]{2,1,0:T(4,128)(2,1)S(1)}, bf16[128,4,128]{2,1,0:T(4,128)(2,1)}, u32[]{:S(2)}) copy-start(bf16[128,4,128]{2,1,0:T(4,128)(2,1)} %slice.313) | copy-start | bytes 393220
  162.7 5.4 %copy-start.1 = (f32[512,1,512]{2,1,0:T(1,128)S(1)}, f32[512,1,512]{2,1,0:T(1,128)}, u32[]{:S(2)}) copy-start(f32[512,1,512]{2,1,0:T(1,128)} %get-tuple-element.103) | copy-start | bytes 3145732
  170.1 36.5 %all-to-all-start.4 = ((bf16[8,64,1,512]{3,1,2,0:T(8,128)(2,1)}), bf16[8,64,1,512]{3,1,2,0:T(8,128)(2,1)}, u32[]{:S(2)}, u32[]{:S(2)}) async-start(bf16[8,64,1,512]{3,1,2,0:T(8,128)(2,1)} %bitcast.239), calls=%async_computation.4 | async-start | bytes 1048576 | tf_op jit(solution)/shard_map/all_to_all | solution.py:142
  174.9 72.1 %reduce-scatter.2.cloned.1.call-start = ((), (), s32[]{:S(2)}) async-start(), calls=%async_computation.9 | async-start | bytes 1310720 | tf_op jit(solution)/shard_map/reduce_scatter | solution.py:127
  185.6 4.9 %copy-start.20 = (bf16[128,4,128]{2,1,0:T(4,128)(2,1)S(1)}, bf16[128,4,128]{2,1,0:T(4,128)(2,1)}, u32[]{:S(2)}) copy-start(bf16[128,4,128]{2,1,0:T(4,128)(2,1)} %slice.329) | copy-start | bytes 393220
  185.6 17.1 %collective-permute-start.4 = (bf16[2048,256]{1,0:T(8,128)(2,1)}, bf16[2048,256]{1,0:T(8,128)(2,1)}, u32[]{:S(2)}, u32[]{:S(2)}) collective-permute-start(bf16[2048,256]{1,0:T(8,128)(2,1)} %fusion.61), channel_id=1, source_target_pairs={{0,1},{1,0},{2,3},{3,2},{4,5},{5,4},{6,7},{7,6},{8,9},{9,8},{10,11... | collective-permute-start | bytes 3145736 | tf_op jit(solution)/shard_map/ppermute | solution.py:10
  202.7 2.8 %collective-permute-start.2 = (bf16[512,512]{1,0:T(8,128)(2,1)}, bf16[512,512]{1,0:T(8,128)(2,1)}, u32[]{:S(2)}, u32[]{:S(2)}) collective-permute-start(bf16[512,512]{1,0:T(8,128)(2,1)} %bitcast.234), channel_id=1, source_target_pairs={{0,1},{1,0},{2,3},{3,2},{4,5},{5,4},{6,7},{7,6},{8,9},{9,8},{10,11... | collective-permute-start | bytes 1572872 | tf_op jit(solution)/shard_map/ppermute | solution.py:10
  226.6 18.8 %all-to-all-start.6 = ((bf16[8,64,1,512]{3,1,2,0:T(8,128)(2,1)}), bf16[8,64,1,512]{3,1,2,0:T(8,128)(2,1)S(1)}, u32[]{:S(2)}, u32[]{:S(2)}) async-start(bf16[8,64,1,512]{3,1,2,0:T(8,128)(2,1)} %bitcast.60), calls=%async_computation.6 | async-start | bytes 1048576 | tf_op jit(solution)/shard_map/all_to_all | solution.py:144
  (17 other events, 49.9 us)
Sparse Core Ops, SparseCore 0:
  205.5 28.9 reduce-scatter.1
where the time goes:
time: 258 us; the launch traced here: 256 us
  waiting for transfers between devices  62.4 us (24%)
  local copies, waits for them, and re-layouts  61.6 us (24%)
  matrix products  44 us (17%)
  starting transfers between devices  32.3 us (13%)
  other arithmetic  21 us (8%)
  blocking collectives  19.9 us (8%)
  between operations  14.5 us (6%)
    all_to_all x1, blocking collectives, body(): lax.all_to_all(to_tokens(key_grad), 'seq', split_axis=0, concat_axis=2, t...  19.9 us
    all_to_all x1, waiting for transfers between devices, body(): lax.all_to_all(to_heads(values), 'seq', split_axis=1, concat_axis=0, tile...  14 us
    all_to_all x1, waiting for transfers between devices, body(): lax.all_to_all(to_heads(out_grad), 'seq', split_axis=1, concat_axis=0, ti...  13.9 us
    all_to_all x1, waiting for transfers between devices, body(): lax.all_to_all(to_heads(key_vectors), 'seq', split_axis=1, concat_axis=0,...  13.2 us
    dot_general x4, matrix products, body(): jnp.einsum('hqk,qhd->khd', dscore, query_block, preferred_element_type=jn...  10.8 us
    all_to_all x1, waiting for transfers between devices, body(): lax.all_to_all(to_tokens(value_grad), 'seq', split_axis=0, concat_axis=2,...  10.8 us
    all_to_all x1, waiting for transfers between devices, body(): lax.all_to_all(to_heads(queries), 'seq', split_axis=1, concat_axis=0, til...  10.3 us
    dot_general x4, matrix products, body(): jnp.einsum('hqk,qhd->khd', probs_low, grad_block, preferred_element_type=...  9.58 us
  transfers between devices with their start and end apart: 13, of which 5 were waited for; matrix products, arithmetic and copies ran while one was open for 48% of the time, Pallas kernels for 0%

commit v1 on v0

--- a/solution.py
+++ b/solution.py
@@ -1,9 +1,22 @@
+import functools
 import jax
 import jax.numpy as jnp
 from jax import lax
 from jax.sharding import PartitionSpec as P
 
 HD = 128
+
+
+def spans_launch(buf, which_axis):
+    g_now = lax.axis_size(which_axis)
+    item_now = jnp.split(buf, g_now, axis=0)
+    work_now = jnp.stack(item_now, axis=0)
+    field_out = lax.all_to_all(work_now, axis_name=which_axis, split_axis=0, concat_axis=0)
+    part_now = jnp.concatenate(field_out, axis=2)
+    return part_now
+
+
+case_define = functools.partial(spans_launch, which_axis="seq")
 
 
 def partner(value, axis, apart):
@@ -141,7 +154,7 @@
     returned = (
         lax.all_to_all(to_tokens(query_grad), "seq", split_axis=0, concat_axis=2, tiled=True),
         lax.all_to_all(to_tokens(key_grad), "seq", split_axis=0, concat_axis=2, tiled=True),
-        lax.all_to_all(to_tokens(value_grad), "seq", split_axis=0, concat_axis=2, tiled=True),
+        case_define(to_tokens(value_grad)),
     )
     return (from_heads(returned[0]), from_heads(returned[1]), from_heads(returned[2]), weight_grad)
 

time: 258 us -> 236 us (0.915)
  waiting for transfers between devices: 62.4 us -> 84 us
  blocking collectives: 19.9 us -> 0 us
  local copies, waits for them, and re-layouts: 61.6 us -> 48.9 us
  matrix products: 44 us -> 32.1 us
  starting transfers between devices: 32.3 us -> 36.5 us
    all_to_all x1 -> x0, blocking collectives: 19.9 us -> none  [body(): lax.all_to_all(to_tokens(key_grad), 'seq', split_axis=0, concat_axis=2, t...]
    all_to_all x1 -> x2, waiting for transfers between devices: 10.8 us -> 24 us  [the longest x1 12.2 us: body(): lax.all_to_all(to_tokens(key_grad), 'seq', split_axis=0, concat_axis=2, t...]
    all_to_all x1, waiting for transfers between devices: 0.01 us -> 8.39 us  [body(): lax.all_to_all(to_tokens(query_grad), 'seq', split_axis=0, concat_axis=2,...]
    slice x5, local copies, waits for them, and re-layouts: 8.26 us -> 2.78 us  [body(): query_block = query_heads[start:stop]]
    unnamed x60 -> x55, local copies, waits for them, and re-layouts: 6.83 us -> 12.3 us
    dot_general x4, matrix products: 10.8 us -> 6.24 us  [body(): jnp.einsum('hqk,qhd->khd', dscore, query_block, preferred_element_type=jn...]
    scatter-add x2, local copies, waits for them, and re-layouts: 6.51 us -> 2.53 us  [body(): key_total.at[low:high]]
    all_to_all x1 -> x2, starting transfers between devices: 3.75 us -> 7.25 us  [the longest x1 3.75 us: spans_launch(): lax.all_to_all(work_now, axis_name=which_axis, split_axis=0, concat_axis=0)]
  transfers between devices with their start and end apart: 13 -> 14, of which waited for: 5 -> 7; matrix products, arithmetic and copies ran while one was open for 48% -> 40% of each run, Pallas kernels for 0% -> 0%
where the time goes in v1:
time: 236 us; the launch traced here: 235 us
  waiting for transfers between devices  84 us (36%)
  local copies, waits for them, and re-layouts  48.9 us (21%)
  starting transfers between devices  36.5 us (15%)
  matrix products  32.1 us (14%)
  other arithmetic  18.6 us (8%)
  between operations  14.7 us (6%)
    all_to_all x1, waiting for transfers between devices, body(): lax.all_to_all(to_heads(values), 'seq', split_axis=1, concat_axis=0, tile...  14 us
    all_to_all x1, waiting for transfers between devices, body(): lax.all_to_all(to_heads(out_grad), 'seq', split_axis=1, concat_axis=0, ti...  13.9 us
    all_to_all x1, waiting for transfers between devices, body(): lax.all_to_all(to_heads(key_vectors), 'seq', split_axis=1, concat_axis=0,...  13.2 us
    unnamed x55, local copies, waits for them, and re-layouts  12.3 us
    all_to_all x1, waiting for transfers between devices, body(): lax.all_to_all(to_tokens(key_grad), 'seq', split_axis=0, concat_axis=2, t...  12.2 us
    all_to_all x1, waiting for transfers between devices, spans_launch(): lax.all_to_all(work_now, axis_name=which_axis, split_axis=0, concat_axis=0)  11.8 us
    all_to_all x1, waiting for transfers between devices, body(): lax.all_to_all(to_heads(queries), 'seq', split_axis=1, concat_axis=0, til...  10.4 us
    all_to_all x1, waiting for transfers between devices, body(): lax.all_to_all(to_tokens(query_grad), 'seq', split_axis=0, concat_axis=2,...  8.39 us
  transfers between devices with their start and end apart: 14, of which 7 were waited for; matrix products, arithmetic and copies ran while one was open for 40% of the time, Pallas kernels for 0%

profile of v1, /device:TPU:0, one launch (start us, length us, event | category | flops | bytes accessed | tf_op | source)
XLA Modules:
  0.0 234.8 jit_solution(16852492152801601704)
XLA Ops:
  9.6 6.5 %all-to-all-start.2 = ((bf16[64,8,512]{2,0,1:T(8,128)(2,1)}), bf16[64,8,512]{2,0,1:T(8,128)(2,1)S(1)}, u32[]{:S(2)}, u32[]{:S(2)}) async-start(bf16[64,8,512]{2,0,1:T(8,128)(2,1)} %bitcast.15), calls=%async_computation.2 | async-start | bytes 1048576 | tf_op jit(solution)/shard_map/all_to_all | solution.py:55
  17.4 14.0 %all-to-all-done.2 = bf16[64,8,512]{2,0,1:T(8,128)(2,1)S(1)} async-done(((bf16[64,8,512]{2,0,1:T(8,128)(2,1)}), bf16[64,8,512]{2,0,1:T(8,128)(2,1)S(1)}, u32[]{:S(2)}, u32[]{:S(2)}) %all-to-all-start.2) | async-done | bytes 524320 | tf_op jit(solution)/shard_map/all_to_all | solution.py:55
  31.4 3.6 %all-to-all-start.3 = ((bf16[64,8,512]{2,0,1:T(8,128)(2,1)}), bf16[64,8,512]{2,0,1:T(8,128)(2,1)S(1)}, u32[]{:S(2)}, u32[]{:S(2)}) async-start(bf16[64,8,512]{2,0,1:T(8,128)(2,1)} %bitcast.24), calls=%async_computation.3 | async-start | bytes 1048576 | tf_op jit(solution)/shard_map/all_to_all | solution.py:56
  36.4 13.9 %all-to-all-done.3 = bf16[64,8,512]{2,0,1:T(8,128)(2,1)S(1)} async-done(((bf16[64,8,512]{2,0,1:T(8,128)(2,1)}), bf16[64,8,512]{2,0,1:T(8,128)(2,1)S(1)}, u32[]{:S(2)}, u32[]{:S(2)}) %all-to-all-start.3) | async-done | bytes 524320 | tf_op jit(solution)/shard_map/all_to_all | solution.py:56
  50.4 3.5 %all-to-all-start = ((bf16[64,8,512]{2,0,1:T(8,128)(2,1)}), bf16[64,8,512]{2,0,1:T(8,128)(2,1)S(1)}, u32[]{:S(2)}, u32[]{:S(2)}) async-start(bf16[64,8,512]{2,0,1:T(8,128)(2,1)} %bitcast.1), calls=%async_computation | async-start | bytes 1048576 | tf_op jit(solution)/shard_map/all_to_all | solution.py:54
  55.9 13.2 %all-to-all-done = bf16[64,8,512]{2,0,1:T(8,128)(2,1)S(1)} async-done(((bf16[64,8,512]{2,0,1:T(8,128)(2,1)}), bf16[64,8,512]{2,0,1:T(8,128)(2,1)S(1)}, u32[]{:S(2)}, u32[]{:S(2)}) %all-to-all-start) | async-done | bytes 524320 | tf_op jit(solution)/shard_map/all_to_all | solution.py:54
  69.1 3.5 %all-to-all-start.1 = ((bf16[64,8,512]{2,0,1:T(8,128)(2,1)}), bf16[64,8,512]{2,0,1:T(8,128)(2,1)S(1)}, u32[]{:S(2)}, u32[]{:S(2)}) async-start(bf16[64,8,512]{2,0,1:T(8,128)(2,1)} %bitcast.10), calls=%async_computation.1 | async-start | bytes 1048576 | tf_op jit(solution)/shard_map/all_to_all | solution.py:53
  77.6 10.4 %all-to-all-done.1 = bf16[64,8,512]{2,0,1:T(8,128)(2,1)S(1)} async-done(((bf16[64,8,512]{2,0,1:T(8,128)(2,1)}), bf16[64,8,512]{2,0,1:T(8,128)(2,1)S(1)}, u32[]{:S(2)}, u32[]{:S(2)}) %all-to-all-start.1) | async-done | bytes 524320 | tf_op jit(solution)/shard_map/all_to_all | solution.py:53
  89.5 4.5 %all-to-all-start.7 = ((bf16[64,8,2048]{2,0,1:T(8,128)(2,1)}), bf16[64,8,2048]{2,0,1:T(8,128)(2,1)}, u32[]{:S(2)}, u32[]{:S(2)}) async-start(bf16[64,8,2048]{2,0,1:T(8,128)(2,1)} %bitcast.70), calls=%async_computation.7 | async-start | bytes 4194304 | tf_op jit(solution)/shard_map/all_to_all | solution.py:131
  124.0 2.2 convolution_bitcast_fusion.3
  132.0 2.3 copy.167
  135.8 2.2 fusion.60
  139.2 3.0 %fusion.57 = (bf16[512,1,512]{2,1,0:T(2,128)(2,1)S(1)}, f32[512,1,512]{2,1,0:T(1,128)}) fusion(pred[]{:T(512)S(6)} %eq.5, bf16[512,2,512]{2,1,0:T(2,128)(2,1)S(1)} %reshape.507), kind=kLoop, calls=%fused_computation.95 | loop fusion | flops 786432 | bytes 2621441 | tf_op jit(solution)/shard_map/convert_element_type | solution.py:119
  150.5 2.9 %fusion.249 = f32[512,2048]{1,0:T(8,128)S(1)} fusion(bf16[512,512]{1,0:T(8,128)(2,1)S(1)} %fusion.62, bf16[512,2048]{1,0:T(8,128)(2,1)} %bitcast.73), kind=kOutput, calls=%fused_computation.237 | convolution fusion | flops 1073741824 | bytes 6815744 | tf_op jit(solution)/shard_map/td,tc->dc/dot_general | solution.py:134
  153.4 2.2 fusion.226
  157.6 3.0 %copy.180 = f32[2048,1,256]{2,0,1:T(8,128)} copy(f32[2048,1,256]{0,2,1:T(8,128)} %get-tuple-element.100) | data formatting | bytes 4194304
  166.9 4.8 %all-to-all-start.4 = ((bf16[8,64,1,512]{3,1,2,0:T(8,128)(2,1)}), bf16[8,64,1,512]{3,1,2,0:T(8,128)(2,1)S(1)}, u32[]{:S(2)}, u32[]{:S(2)}) async-start(bf16[8,64,1,512]{3,1,2,0:T(8,128)(2,1)} %bitcast.268), calls=%async_computation.4 | async-start | bytes 1048576 | tf_op jit(solution)/shard_map/all_to_all | solution.py:155
  172.4 2.4 %fusion.63 = bf16[512,512]{1,0:T(8,128)(2,1)} fusion(f32[512,1,512]{2,1,0:T(1,128)} %get-tuple-element.105, bf16[512,512]{1,0:T(8,128)(2,1)} %collective-permute-done.2), kind=kLoop, calls=%fused_computation.103 | loop fusion | flops 786432 | bytes 2097152 | tf_op jit(solution)/shard_map/convert_element_type | solution.py:124
  175.4 2.6 %fusion.8 = bf16[2048,256]{1,0:T(8,128)(2,1)} fusion(bf16[2048,256]{1,0:T(8,128)(2,1)} %collective-permute-done.4, f32[2048,1,256]{2,0,1:T(8,128)S(1)} %copy-done, f32[2048,1,256]{2,0,1:T(8,128)S(1)} %copy.181, pred[]{:T(512)S(6)} %eq.5), kind=kLoop, calls=%fused_computation.9 | loop fusion | flops 2097152 | bytes 6291457 | tf_op jit(solution)/shard_map/convert_element_type | solution.py:141
  178.7 8.4 %all-to-all-done.4 = bf16[8,64,1,512]{3,1,2,0:T(8,128)(2,1)S(1)} async-done(((bf16[8,64,1,512]{3,1,2,0:T(8,128)(2,1)}), bf16[8,64,1,512]{3,1,2,0:T(8,128)(2,1)S(1)}, u32[]{:S(2)}, u32[]{:S(2)}) %all-to-all-start.4) | async-done | bytes 524320 | tf_op jit(solution)/shard_map/all_to_all | solution.py:155
  187.1 3.5 %all-to-all-start.5 = ((bf16[8,64,1,512]{3,1,2,0:T(8,128)(2,1)}), bf16[8,64,1,512]{3,1,2,0:T(8,128)(2,1)S(1)}, u32[]{:S(2)}, u32[]{:S(2)}) async-start(bf16[8,64,1,512]{3,1,2,0:T(8,128)(2,1)} %bitcast.275), calls=%async_computation.5 | async-start | bytes 1048576 | tf_op jit(solution)/shard_map/all_to_all | solution.py:156
  193.7 12.2 %all-to-all-done.5 = bf16[8,64,1,512]{3,1,2,0:T(8,128)(2,1)S(1)} async-done(((bf16[8,64,1,512]{3,1,2,0:T(8,128)(2,1)}), bf16[8,64,1,512]{3,1,2,0:T(8,128)(2,1)S(1)}, u32[]{:S(2)}, u32[]{:S(2)}) %all-to-all-start.5) | async-done | bytes 524320 | tf_op jit(solution)/shard_map/all_to_all | solution.py:156
  205.8 3.8 %all-to-all-start.6 = ((bf16[8,1,64,1,512]{4,2,3,1,0:T(8,128)(2,1)}), bf16[8,1,64,1,512]{4,2,3,1,0:T(8,128)(2,1)S(1)}, u32[]{:S(2)}, u32[]{:S(2)}) async-start(bf16[8,1,64,1,512]{4,2,3,1,0:T(8,128)(2,1)} %fusion.126), calls=%async_computation.6 | async-start | bytes 1048576 | tf_op jit(solution)/shard_map/all_to_all | solution.py:14
  212.8 11.8 %all-to-all-done.6 = bf16[8,1,64,1,512]{4,2,3,1,0:T(8,128)(2,1)S(1)} async-done(((bf16[8,1,64,1,512]{4,2,3,1,0:T(8,128)(2,1)}), bf16[8,1,64,1,512]{4,2,3,1,0:T(8,128)(2,1)S(1)}, u32[]{:S(2)}, u32[]{:S(2)}) %all-to-all-start.6) | async-done | bytes 524320 | tf_op jit(solution)/shard_map/all_to_all | solution.py:14
  (155 shorter events, 79.8 us)
Async XLA Ops:
  7.2 8.9 %copy-start.6 = (bf16[1,128,2048]{2,1,0:T(8,128)(2,1)S(1)}, bf16[1,128,2048]{2,1,0:T(8,128)(2,1)}, u32[]{:S(2)}) copy-start(bf16[1,128,2048]{2,1,0:T(8,128)(2,1)} %param.24) | copy-start | bytes 1572868
  9.6 25.5 %copy-start.7 = (bf16[1,128,2048]{2,1,0:T(8,128)(2,1)S(1)}, bf16[1,128,2048]{2,1,0:T(8,128)(2,1)}, u32[]{:S(2)}) copy-start(bf16[1,128,2048]{2,1,0:T(8,128)(2,1)} %param.22) | copy-start | bytes 1572868
  9.6 21.8 %all-to-all-start.2 = ((bf16[64,8,512]{2,0,1:T(8,128)(2,1)}), bf16[64,8,512]{2,0,1:T(8,128)(2,1)S(1)}, u32[]{:S(2)}, u32[]{:S(2)}) async-start(bf16[64,8,512]{2,0,1:T(8,128)(2,1)} %bitcast.15), calls=%async_computation.2 | async-start | bytes 1048576 | tf_op jit(solution)/shard_map/all_to_all | solution.py:55
  31.4 22.4 %copy-start.8 = (bf16[1,128,2048]{2,1,0:T(8,128)(2,1)S(1)}, bf16[1,128,2048]{2,1,0:T(8,128)(2,1)}, u32[]{:S(2)}) copy-start(bf16[1,128,2048]{2,1,0:T(8,128)(2,1)} %param.21) | copy-start | bytes 1572868
  31.4 18.9 %all-to-all-start.3 = ((bf16[64,8,512]{2,0,1:T(8,128)(2,1)}), bf16[64,8,512]{2,0,1:T(8,128)(2,1)S(1)}, u32[]{:S(2)}, u32[]{:S(2)}) async-start(bf16[64,8,512]{2,0,1:T(8,128)(2,1)} %bitcast.24), calls=%async_computation.3 | async-start | bytes 1048576 | tf_op jit(solution)/shard_map/all_to_all | solution.py:56
  50.4 18.8 %all-to-all-start = ((bf16[64,8,512]{2,0,1:T(8,128)(2,1)}), bf16[64,8,512]{2,0,1:T(8,128)(2,1)S(1)}, u32[]{:S(2)}, u32[]{:S(2)}) async-start(bf16[64,8,512]{2,0,1:T(8,128)(2,1)} %bitcast.1), calls=%async_computation | async-start | bytes 1048576 | tf_op jit(solution)/shard_map/all_to_all | solution.py:54
  69.1 18.8 %all-to-all-start.1 = ((bf16[64,8,512]{2,0,1:T(8,128)(2,1)}), bf16[64,8,512]{2,0,1:T(8,128)(2,1)S(1)}, u32[]{:S(2)}, u32[]{:S(2)}) async-start(bf16[64,8,512]{2,0,1:T(8,128)(2,1)} %bitcast.10), calls=%async_computation.1 | async-start | bytes 1048576 | tf_op jit(solution)/shard_map/all_to_all | solution.py:53
  74.1 23.6 %collective-permute-start.1 = (bf16[512,512]{1,0:T(8,128)(2,1)S(1)}, bf16[512,512]{1,0:T(8,128)(2,1)}, u32[]{:S(2)}, u32[]{:S(2)}) collective-permute-start(bf16[512,512]{1,0:T(8,128)(2,1)S(1)} %bitcast.263), channel_id=1, source_target_pairs={{0,1},{1,0},{2,3},{3,2},{4,5},{5,4},{6,7},{7,6},{8,9},{9,8},{10,11... | collective-permute-start | bytes 1572872 | tf_op jit(solution)/shard_map/ppermute | solution.py:23
  76.6 22.7 %collective-permute-start = (bf16[512,512]{1,0:T(8,128)(2,1)S(1)}, bf16[512,512]{1,0:T(8,128)(2,1)S(1)}, u32[]{:S(2)}, u32[]{:S(2)}) collective-permute-start(bf16[512,512]{1,0:T(8,128)(2,1)S(1)} %bitcast.264), channel_id=1, source_target_pairs={{0,1},{1,0},{2,3},{3,2},{4,5},{5,4},{6,7},{7,6},{8,9},{9,8},{10,11... | collective-permute-start | bytes 1572872 | tf_op jit(solution)/shard_map/ppermute | solution.py:23
  89.5 61.1 %all-to-all-start.7 = ((bf16[64,8,2048]{2,0,1:T(8,128)(2,1)}), bf16[64,8,2048]{2,0,1:T(8,128)(2,1)}, u32[]{:S(2)}, u32[]{:S(2)}) async-start(bf16[64,8,2048]{2,0,1:T(8,128)(2,1)} %bitcast.70), calls=%async_computation.7 | async-start | bytes 4194304 | tf_op jit(solution)/shard_map/all_to_all | solution.py:131
  106.1 12.1 %copy-start.3 = (f32[4,128,256]{1,2,0:T(8,128)}, f32[4,128,256]{1,2,0:T(8,128)S(1)}, u32[]{:S(2)}) copy-start(f32[4,128,256]{1,2,0:T(8,128)S(1)} %convolution_bitcast_fusion.9) | copy-start | bytes 1572868
  106.4 10.2 %copy-start.2 = (f32[4,128,256]{1,2,0:T(8,128)}, f32[4,128,256]{1,2,0:T(8,128)S(1)}, u32[]{:S(2)}) copy-start(f32[4,128,256]{1,2,0:T(8,128)S(1)} %convolution_bitcast_fusion.10) | copy-start | bytes 1572868
  139.0 3.2 %copy-start.14 = (bf16[256,4,128]{2,1,0:T(4,128)(2,1)S(1)}, bf16[256,4,128]{2,1,0:T(4,128)(2,1)}, u32[]{:S(2)}) copy-start(bf16[256,4,128]{2,1,0:T(4,128)(2,1)} %slice.335) | copy-start | bytes 786436
  139.0 10.3 %collective-permute-start.3 = (bf16[512,512]{1,0:T(8,128)(2,1)}, bf16[512,512]{1,0:T(8,128)(2,1)}, u32[]{:S(2)}, u32[]{:S(2)}) collective-permute-start(bf16[512,512]{1,0:T(8,128)(2,1)} %bitcast.260), channel_id=1, source_target_pairs={{0,1},{1,0},{2,3},{3,2},{4,5},{5,4},{6,7},{7,6},{8,9},{9,8},{10,11... | collective-permute-start | bytes 1572872 | tf_op jit(solution)/shard_map/ppermute | solution.py:23
  142.2 3.2 %copy-start.13 = (bf16[256,4,128]{2,1,0:T(4,128)(2,1)S(1)}, bf16[256,4,128]{2,1,0:T(4,128)(2,1)}, u32[]{:S(2)}) copy-start(bf16[256,4,128]{2,1,0:T(4,128)(2,1)} %slice.327) | copy-start | bytes 786436
  144.1 3.2 %copy-start.15 = (bf16[256,4,128]{2,1,0:T(4,128)(2,1)S(1)}, bf16[256,4,128]{2,1,0:T(4,128)(2,1)}, u32[]{:S(2)}) copy-start(bf16[256,4,128]{2,1,0:T(4,128)(2,1)} %slice.319) | copy-start | bytes 786436
  145.0 27.4 %collective-permute-start.2 = (bf16[512,512]{1,0:T(8,128)(2,1)}, bf16[512,512]{1,0:T(8,128)(2,1)}, u32[]{:S(2)}, u32[]{:S(2)}) collective-permute-start(bf16[512,512]{1,0:T(8,128)(2,1)} %bitcast.261), channel_id=1, source_target_pairs={{0,1},{1,0},{2,3},{3,2},{4,5},{5,4},{6,7},{7,6},{8,9},{9,8},{10,11... | collective-permute-start | bytes 1572872 | tf_op jit(solution)/shard_map/ppermute | solution.py:23
  160.5 3.0 %copy-start.12 = (bf16[256,4,128]{2,1,0:T(4,128)(2,1)S(1)}, bf16[256,4,128]{2,1,0:T(4,128)(2,1)}, u32[]{:S(2)}) copy-start(bf16[256,4,128]{2,1,0:T(4,128)(2,1)} %copy-done.11) | copy-start | bytes 786436
  161.7 13.6 %collective-permute-start.4 = (bf16[2048,256]{1,0:T(8,128)(2,1)}, bf16[2048,256]{1,0:T(8,128)(2,1)}, u32[]{:S(2)}, u32[]{:S(2)}) collective-permute-start(bf16[2048,256]{1,0:T(8,128)(2,1)} %fusion.61), channel_id=1, source_target_pairs={{0,1},{1,0},{2,3},{3,2},{4,5},{5,4},{6,7},{7,6},{8,9},{9,8},{10,11... | collective-permute-start | bytes 3145736 | tf_op jit(solution)/shard_map/ppermute | solution.py:23
  166.9 20.1 %all-to-all-start.4 = ((bf16[8,64,1,512]{3,1,2,0:T(8,128)(2,1)}), bf16[8,64,1,512]{3,1,2,0:T(8,128)(2,1)S(1)}, u32[]{:S(2)}, u32[]{:S(2)}) async-start(bf16[8,64,1,512]{3,1,2,0:T(8,128)(2,1)} %bitcast.268), calls=%async_computation.4 | async-start | bytes 1048576 | tf_op jit(solution)/shard_map/all_to_all | solution.py:155
  171.7 54.5 %reduce-scatter.2.cloned.1.call-start = ((), (), s32[]{:S(2)}) async-start(), calls=%async_computation.9 | async-start | bytes 1310720 | tf_op jit(solution)/shard_map/reduce_scatter | solution.py:140
  171.7 3.6 %copy-start = (f32[2048,1,256]{2,0,1:T(8,128)S(1)}, f32[2048,1,256]{2,0,1:T(8,128)}, u32[]{:S(2)}) copy-start(f32[2048,1,256]{2,0,1:T(8,128)} %copy.180) | copy-start | bytes 6291460
  187.1 18.8 %all-to-all-start.5 = ((bf16[8,64,1,512]{3,1,2,0:T(8,128)(2,1)}), bf16[8,64,1,512]{3,1,2,0:T(8,128)(2,1)S(1)}, u32[]{:S(2)}, u32[]{:S(2)}) async-start(bf16[8,64,1,512]{3,1,2,0:T(8,128)(2,1)} %bitcast.275), calls=%async_computation.5 | async-start | bytes 1048576 | tf_op jit(solution)/shard_map/all_to_all | solution.py:156
  205.8 18.8 %all-to-all-start.6 = ((bf16[8,1,64,1,512]{4,2,3,1,0:T(8,128)(2,1)}), bf16[8,1,64,1,512]{4,2,3,1,0:T(8,128)(2,1)S(1)}, u32[]{:S(2)}, u32[]{:S(2)}) async-start(bf16[8,1,64,1,512]{4,2,3,1,0:T(8,128)(2,1)} %fusion.126), calls=%async_computation.6 | async-start | bytes 1048576 | tf_op jit(solution)/shard_map/all_to_all | solution.py:14
  (12 other events, 18.7 us)
Sparse Core Ops, SparseCore 0:
  178.2 29.1 reduce-scatter.1
